TPU v7x, 512 devices: a whole 4x4x16 slice. The times are simulated.
512 devices in a mesh: layer: 4 (over z_lo), row: 8 (over z_hi, core), col: 16 (over y, x).
Axes of the slice: x: 4, y: 4, z: 16 (z_hi: 4, z_lo: 4; z = z_hi * 4 + z_lo), core: 2. Of those that a mesh axis runs over, the one named last changes fastest.
Arguments:
- panels: float32 [16384, 8192], P('row', ('layer', 'col')), may hold values from -0.0625 to 0.0625
- eigvecs: float32 [8192, 2048], P(('layer', 'row'), 'col'), may hold values from -6 to 6
Outputs:
- result: float32 [16384, 2048], P('row', 'col')
All inputs are finite; a program needn't handle non-finite values.
Results may differ from a plain program's by a relative error of at most 0.0001.
Values sent between devices are 32-bit elements; how exact they have to be, the bound alone decides.
A program may use at most 64 MiB of HBM per device.

v0:
```python
import jax
import jax.numpy as jnp
from jax import lax
from jax.sharding import PartitionSpec as P


def in_order(pieces, dim):
    dims = list(pieces.shape[1:])
    dims[dim] *= pieces.shape[0]
    return jnp.moveaxis(pieces, 0, dim).reshape(dims)


def from_everyone(x, axis):
    devices = lax.axis_size(axis)
    return lax.all_to_all(jnp.broadcast_to(x[None], (devices, *x.shape)), axis, 0, 0, tiled=True)


def collect(x, axis, dim):
    return in_order(from_everyone(x, axis), dim)


def cut_along(x, dim, devices):
    before, after = (x.shape[:dim], x.shape[dim + 1 :])
    return jnp.moveaxis(x.reshape(*before, devices, -1, *after), dim, 0)


def sent_and_summed(x, axis, dim):
    devices = lax.axis_size(axis)
    pieces = lax.all_to_all(cut_along(x, dim, devices), axis, 0, 0, tiled=True)
    return jnp.sum(pieces, axis=0)


def local(panels, eigvecs):
    layer_vecs = collect(eigvecs, "row", 0)
    partial_sum = jnp.dot(
        lax.all_gather(panels, "col", axis=1, tiled=True),
        layer_vecs,
        preferred_element_type=jnp.float32,
        precision=lax.Precision.HIGHEST,
    )
    shares = sent_and_summed(partial_sum, "layer", 0)
    result = collect(shares, "layer", 0)
    return result


def solution(mesh):
    in_specs = (P("row", ("layer", "col")), P(("layer", "row"), "col"))
    out_specs = P("row", "col")
    return jax.shard_map(local, mesh=mesh, in_specs=in_specs, out_specs=out_specs, check_vma=False)
```

profile of v0, /device:TPU:24, one launch (start us, length us, event | category | flops | bytes accessed | tf_op | source)
XLA Modules:
  0.0 229.4 jit_solution(10799555206878883589)
XLA Ops:
  6.5 0.0 all-gather.2.cloned.1.call-start
  6.5 0.7 all-gather.2.cloned.1.call-update
  7.3 1.0 broadcast_in_dim.4
  8.2 65.8 %all_to_all.15 = f32[8,256,128]{2,1,0:T(8,128)S(1)} all-to-all(f32[8,256,128]{2,1,0:T(8,128)S(1)} %broadcast_in_dim.4), channel_id=1, replica_groups=mesh['layer'=4,'row'=8,'col'=16] {'row'}, dimensions={0} | all-to-all | bytes 2097152 | tf_op jit(solution)/shard_map/all_to_all | solution.py:15
  74.0 75.3 %all-gather.2.cloned.1.call-done = f32[2048,2048]{1,0:T(8,128)} async-done(((f32[2048,128]{1,0:T(8,128)}), f32[2048,2048]{1,0:T(8,128)}) %all-gather.2.cloned.1.call-update) | async-done | bytes 16777232 | tf_op jit(solution)/shard_map/all_gather | solution.py:36
  149.3 15.9 %fusion = f32[4,512,128]{2,1,0:T(8,128)S(1)} fusion(f32[4,512,2048]{2,1,0:T(8,128)} %bitcast.7, f32[2048,128,1]{1,0,2:T(8,128)S(1)} %bitcast.8), kind=kOutput, calls=%fused_computation | convolution fusion | flops 6442450944 | bytes 18874368 | tf_op jit(solution)/shard_map/dot_general | solution.py:35
  165.2 29.0 %all_to_all.16 = f32[4,512,128]{2,1,0:T(8,128)S(1)} all-to-all(f32[4,512,128]{2,1,0:T(8,128)S(1)} %fusion), channel_id=1, replica_groups=mesh['layer'=4,'row'=8,'col'=16] {'layer'}, dimensions={0} | all-to-all | bytes 2097152 | tf_op jit(solution)/shard_map/all_to_all | solution.py:29
  194.2 0.1 reduce_sum.9
  194.3 0.1 broadcast_in_dim.5
  194.4 27.2 %all_to_all.17 = f32[4,512,128]{2,1,0:T(8,128)S(1)} all-to-all(f32[4,512,128]{2,1,0:T(8,128)S(1)} %broadcast_in_dim.5), channel_id=1, replica_groups=mesh['layer'=4,'row'=8,'col'=16] {'layer'}, dimensions={0} | all-to-all | bytes 2097152 | tf_op jit(solution)/shard_map/all_to_all | solution.py:15
  221.6 1.0 copy.4
Async XLA Ops:
  6.5 142.8 %all-gather.2.cloned.1.call-start = ((), (), s32[]{:S(2)}) async-start(), calls=%async_computation.3 | async-start | bytes 17825792 | tf_op jit(solution)/shard_map/all_gather | solution.py:36
Sparse Core Ops, SparseCore 0:
  10.3 138.9 all-gather.1
where the time goes:
time: 230 us; the launch traced here: 229 us
  blocking collectives  122 us (53%)
  waiting for transfers between devices  76 us (33%)
  matrix products  15.9 us (7%)
  between operations  13.4 us (6%)
    all_to_all x2, blocking collectives, from_everyone(): lax.all_to_all(jnp.broadcast_to(x[None], (devices, *x.shape)), axis, 0, 0...  93 us
    all_gather x1, waiting for transfers between devices, local(): lax.all_gather(panels, 'col', axis=1, tiled=True)  75.3 us
    all_to_all x1, blocking collectives, sent_and_summed(): pieces = lax.all_to_all(cut_along(x, dim, devices), axis, 0, 0, tiled=True)  29 us
    dot_general x1, matrix products, local(): jnp.dot(lax.all_gather(panels, 'col', axis=1, tiled=True), layer_vecs, pr...  15.9 us
  transfers between devices with their start and end apart: 1, of which 1 were waited for; matrix products, arithmetic and copies ran while one was open for 0% of the time, Pallas kernels for 0%

commit v1 on v0

v1 whole, which is shorter than its diff:
```python
import jax
import jax.numpy as jnp
from jax import lax
from jax.experimental import pallas as pl
from jax.experimental.pallas import tpu as pltpu
from jax.sharding import PartitionSpec as P

MESH = pl.DeviceIdType.MESH
CHUNKS = 8
BK = 128


def remote(src, dst, send, recv, device):
    return pltpu.make_async_remote_copy(src_ref=src, dst_ref=dst, send_sem=send, recv_sem=recv, device_id=device, device_id_type=MESH)


def drain(ref, sem):
    pltpu.make_async_copy(ref, ref, sem).wait()


def halves(x):
    hi = x.astype(jnp.bfloat16)
    return hi, (x - hi.astype(jnp.float32)).astype(jnp.bfloat16)


def kernel(
    a_ref, e_ref, o_ref,
    a_low, a_high, a_far, b_first, b_second, b_far, b_all, b_cat, prod,
    half_up, half_down, sum_up, sum_down, z_mine, z_in, z_pair, z_other,
    as_up, as_down, ar_low, ar_high, as_far, ar_far,
    bs_first, br_first, bs_second, br_second, bs_far, br_far, bs_plane, br_plane,
    ps_half, pr_up, pr_down, ps_up, ps_down, qr_up, qr_down,
    zs_in, zr_in, zs_pair, zr_pair, zs_out, zr_out,
):
    layer, row, col = lax.axis_index("layer"), lax.axis_index("row"), lax.axis_index("col")
    zh, core = lax.div(row, 2), lax.rem(row, 2)
    y, x = lax.div(col, 4), lax.rem(col, 4)
    ga = x + core * (y - x)
    gb = y + core * (x - y)

    def at(a, b):
        return {"col": (1 - core) * (b * 4 + a) + core * (a * 4 + b)}

    a_up, a_down = at(lax.rem(ga + 1, 4), gb), at(lax.rem(ga + 3, 4), gb)
    b_up, b_down = at(ga, lax.rem(gb + 1, 4)), at(ga, lax.rem(gb + 3, 4))
    step = 1 - 2 * core
    zh_first, zh_second = lax.rem(zh + step + 4, 4), lax.rem(zh - step + 4, 4)
    z_first, z_second = {"row": zh_first * 2 + core}, {"row": zh_second * 2 + core}
    outer = jnp.logical_or(layer == 0, layer == 3)
    inner = jnp.logical_not(outer)
    z_inner = {"layer": 1 + lax.div(layer, 2)}
    z_partner = {"layer": lax.rem(3 - layer, 4)}
    z_outer = {"layer": lax.rem(3 * layer + 1, 4)}

    barrier = pltpu.get_barrier_semaphore()

    def greet(device):
        pl.semaphore_signal(barrier, inc=1, device_id=device, device_id_type=MESH)

    for device in (a_up, a_down, b_up, b_down, z_first, z_second):
        greet(device)

    @pl.when(outer)
    def _():
        greet(z_inner)

    @pl.when(inner)
    def _():
        greet(z_partner)
        greet(z_outer)

    @pl.when(core == 0)
    def _():
        for yy in range(4):
            greet({"row": zh * 2 + 1, "col": yy * 4 + x})
        for d in range(1, 4):
            greet({"row": zh * 2, "col": lax.rem(y + d, 4) * 4 + x})

    @pl.when(core == 1)
    def _():
        for d in range(1, 4):
            greet({"row": zh * 2 + lax.div(x, 2), "col": y * 4 + lax.rem(x + d, 4)})

        @pl.when(x < 2)
        def _():
            greet({"row": zh * 2})

    pl.semaphore_wait(barrier, 6 + (2 - outer.astype(jnp.int32)) + 3 + core + 2 - core * lax.div(x, 2))

    firsts = [remote(e_ref.at[h], b_first.at[h], bs_first.at[h], br_first.at[h], z_first) for h in range(2)]
    seconds = [remote(e_ref.at[h], b_second.at[h], bs_second.at[h], br_second.at[h], z_second) for h in range(2)]
    b_fars = [remote(b_first.at[h], b_far.at[h], bs_far.at[h], br_far.at[h], z_first) for h in range(2)]
    half = a_ref.shape[0] // 2
    rows = [pl.ds(h * half, half) for h in range(2)]
    ups = [remote(a_ref.at[rows[h]], a_low.at[rows[h]], as_up.at[h], ar_low.at[h], a_up) for h in range(2)]
    downs = [remote(a_ref.at[rows[h]], a_high.at[rows[h]], as_down.at[h], ar_high.at[h], a_down) for h in range(2)]
    far_up = remote(a_low.at[rows[0]], a_far.at[rows[0]], as_far.at[0], ar_far.at[0], a_up)
    far_down = remote(a_high.at[rows[1]], a_far.at[rows[1]], as_far.at[1], ar_far.at[1], a_down)

    for c in firsts:
        c.start()
    ups[0].start()
    downs[1].start()
    ups[1].start()
    downs[0].start()

    ends = []

    def either(own, copy, local):
        @pl.when(own)
        def _():
            local.start()

        @pl.when(jnp.logical_not(own))
        def _():
            copy.start()

        def end():
            @pl.when(jnp.logical_not(own))
            def _():
                copy.wait_send()

        ends.append(end)

    def in_plane(src, source, k):
        dst = b_all.at[pl.ds(2 * core, 2), y]
        either(
            jnp.logical_and(core == 0, source == y),
            remote(src, dst, bs_plane.at[3 * k], br_plane.at[y], {"row": zh * 2, "col": source * 4 + x}),
            pltpu.make_async_copy(src, dst, br_plane.at[y]),
        )
        for q in range(2):
            dst = b_all.at[source, x]
            either(
                jnp.logical_and(core == 1, x == 2 * core + q),
                remote(src.at[q], dst, bs_plane.at[3 * k + 1 + q], br_plane.at[x], {"row": zh * 2 + 1, "col": y * 4 + 2 * core + q}),
                pltpu.make_async_copy(src.at[q], dst, br_plane.at[x]),
            )

    in_plane(e_ref, zh, 0)
    for h in range(2):
        firsts[h].wait_recv()
        b_fars[h].start()
        seconds[h].start()
    in_plane(b_first, zh_second, 1)
    ups[0].wait_recv()
    far_up.start()
    downs[1].wait_recv()
    far_down.start()
    for h in range(2):
        seconds[h].wait_recv()
    in_plane(b_second, zh_first, 2)
    for h in range(2):
        b_fars[h].wait_recv()
    in_plane(b_far, lax.rem(zh + 2, 4), 3)

    for j in range(4):
        n = lax.rem(gb + j, 4)
        drain(b_all.at[:, n], br_plane.at[n])
        for i in range(4):
            hi, lo = halves(b_all[lax.rem(ga + i, 4), n])
            cols = pl.ds(j * BK, BK)
            b_cat[pl.ds(i * BK, BK), cols] = hi
            b_cat[pl.ds(512 + i * BK, BK), cols] = lo
            b_cat[pl.ds(1024 + i * BK, BK), cols] = hi
    ups[1].wait_recv()
    downs[0].wait_recv()
    far_up.wait_recv()
    far_down.wait_recv()

    size = a_ref.shape[0] // CHUNKS
    part = size // 2

    def span(m):
        return pl.ds(pl.multiple_of(m * size, size), size)

    def top(m):
        return pl.ds(pl.multiple_of(m * size, part), part)

    def bottom(m):
        return pl.ds(pl.multiple_of(m * size + part, part), part)

    def multiply(m):
        parts = [halves(ref[span(m), :]) for ref in (a_ref, a_high, a_far, a_low)]
        his, los = [p[0] for p in parts], [p[1] for p in parts]
        left = jnp.concatenate(his + his + los, axis=1)
        out = jnp.dot(left, b_cat[...], preferred_element_type=jnp.float32)
        for j in range(4):
            prod[j, span(m), :] = out[:, j * BK:(j + 1) * BK]
        remote(prod.at[2, top(m)], half_up.at[m], ps_half, pr_up.at[m], b_up).start()
        remote(prod.at[2, bottom(m)], half_down.at[m], ps_half, pr_down.at[m], b_down).start()
        remote(prod.at[1, bottom(m)], sum_up.at[bottom(m)], ps_up, qr_up.at[m], b_up).start()
        remote(prod.at[3, top(m)], sum_down.at[top(m)], ps_down, qr_down.at[m], b_down).start()

    def pass_on(m):
        drain(half_up.at[m], pr_up.at[m])
        prod[1, top(m), :] += half_up[m]
        remote(prod.at[1, top(m)], sum_up.at[top(m)], ps_up, qr_up.at[m], b_up).start()
        drain(half_down.at[m], pr_down.at[m])
        prod[3, bottom(m), :] += half_down[m]
        remote(prod.at[3, bottom(m)], sum_down.at[bottom(m)], ps_down, qr_down.at[m], b_down).start()

    def close_layer(m):
        drain(sum_up.at[span(m)], qr_up.at[m])
        drain(sum_down.at[span(m)], qr_down.at[m])
        z_mine[span(m), :] = prod[0, span(m), :] + (sum_up[span(m), :] + sum_down[span(m), :])

        @pl.when(outer)
        def _():
            remote(z_mine.at[span(m)], z_in.at[span(m)], zs_in, zr_in.at[m], z_inner).start()

    def pair_up(m):
        drain(z_in.at[span(m)], zr_in.at[m])
        z_pair[span(m), :] = z_mine[span(m), :] + z_in[span(m), :]
        remote(z_pair.at[span(m)], z_other.at[span(m)], zs_pair, zr_pair.at[m], z_partner).start()

    def finish(m):
        drain(z_other.at[span(m)], zr_pair.at[m])
        o_ref[span(m), :] = z_pair[span(m), :] + z_other[span(m), :]
        remote(o_ref.at[span(m)], o_ref.at[span(m)], zs_out, zr_out.at[m], z_outer).start()

    lags = (0, 1, 2, 4, 6)

    def body(t, carry):
        for stage, lag, cond in ((multiply, 0, None), (pass_on, 1, None), (close_layer, 2, None), (pair_up, 4, inner), (finish, 6, inner)):
            m = t - lag
            ok = jnp.logical_and(m >= 0, m < CHUNKS)
            if cond is not None:
                ok = jnp.logical_and(ok, cond)
            pl.when(ok)(lambda stage=stage, m=m: stage(m))
        return carry

    lax.fori_loop(0, CHUNKS + lags[-1], body, 0)

    @pl.when(outer)
    def _():
        for m in range(CHUNKS):
            rows_m = pl.ds(m * size, size)
            drain(o_ref.at[rows_m], zr_out.at[m])
        drain(z_mine, zs_in)

    @pl.when(inner)
    def _():
        drain(z_pair, zs_pair)
        drain(o_ref, zs_out)

    drain(prod.at[2], ps_half)
    drain(prod.at[1], ps_up)
    drain(prod.at[3], ps_down)
    for c in firsts + seconds + b_fars + ups + downs + [far_up, far_down]:
        c.wait_send()
    for end in ends:
        end()


def local(panels, eigvecs):
    m, f32 = panels.shape[0], jnp.float32
    whole = pltpu.VMEM((m, BK), f32)
    block = pltpu.VMEM((2, BK, BK), f32)
    dma = pltpu.SemaphoreType.DMA
    part = pltpu.VMEM((CHUNKS, m // CHUNKS // 2, BK), f32)
    return pl.pallas_call(
        kernel,
        out_shape=jax.ShapeDtypeStruct((m, BK), f32),
        in_specs=[pl.BlockSpec(memory_space=pltpu.VMEM)] * 2,
        out_specs=pl.BlockSpec(memory_space=pltpu.VMEM),
        scratch_shapes=[
            whole, whole, whole, block, block, block,
            pltpu.VMEM((4, 4, BK, BK), f32), pltpu.VMEM((12 * BK, 4 * BK), jnp.bfloat16), pltpu.VMEM((4, m, BK), f32),
            part, part, whole, whole, whole, whole, whole, whole,
            dma((2,)), dma((2,)), dma((2,)), dma((2,)), dma((2,)), dma((2,)),
            dma((2,)), dma((2,)), dma((2,)), dma((2,)), dma((2,)), dma((2,)), dma((12,)), dma((4,)),
            dma, dma((CHUNKS,)), dma((CHUNKS,)), dma, dma, dma((CHUNKS,)), dma((CHUNKS,)),
            dma, dma((CHUNKS,)), dma, dma((CHUNKS,)), dma, dma((CHUNKS,)),
        ],
        compiler_params=pltpu.CompilerParams(collective_id=0, has_side_effects=True),
        name="panels_by_vectors",
    )(panels, eigvecs.reshape(2, BK, BK))


def solution(mesh):
    in_specs = (P("row", ("layer", "col")), P(("layer", "row"), "col"))
    return jax.shard_map(local, mesh=mesh, in_specs=in_specs, out_specs=P("row", "col"), check_vma=False)
```

time: 230 us -> 88.7 us (0.39)
  blocking collectives: 122 us -> 0 us
  Pallas kernels: 0 us -> 85.7 us
  waiting for transfers between devices: 76 us -> 0 us
  matrix products: 15.9 us -> 0 us
  between operations: 13.4 us -> 0.01 us
    all_to_all x3 -> x0, blocking collectives: 122 us -> none  [the longest x2 93 us: from_everyone(): lax.all_to_all(jnp.broadcast_to(x[None], (devices, *x.shape)), axis, 0, 0...]
    pallas_call x0 -> x1, Pallas kernels: none -> 85.7 us  [local(): pl.pallas_call(kernel, out_shape=jax.ShapeDtypeStruct((m, BK), f32), in_s...]
    all_gather x1 -> x0, waiting for transfers between devices: 75.3 us -> none  [local(): lax.all_gather(panels, 'col', axis=1, tiled=True)]
    dot_general x1 -> x0, matrix products: 15.9 us -> none  [local(): jnp.dot(lax.all_gather(panels, 'col', axis=1, tiled=True), layer_vecs, pr...]
  transfers between devices with their start and end apart: 1 -> 0, of which waited for: 1 -> 0; matrix products, arithmetic and copies ran while one was open for 0% -> 0% of each run, Pallas kernels for 0% -> 0%
where the time goes in v1:
time: 88.7 us; the launch traced here: 88 us
  Pallas kernels  85.7 us (97%)
  local copies, waits for them, and re-layouts  2.26 us (3%)
    pallas_call x1, Pallas kernels, local(): pl.pallas_call(kernel, out_shape=jax.ShapeDtypeStruct((m, BK), f32), in_s...  85.7 us
    unnamed x1, local copies, waits for them, and re-layouts  2.26 us

profile of v1, /device:TPU:24, one launch (start us, length us, event | category | flops | bytes accessed | tf_op | source)
XLA Modules:
  0.0 88.0 jit_solution(11637094820217332292)
XLA Ops:
  0.0 85.7 %panels_by_vectors.1 = f32[2048,128]{1,0:T(8,128)} custom-call(f32[2048,128]{1,0:T(8,128)} %a_ref.1, f32[2,128,128]{2,1,0:T(8,128)} %bitcast.1), custom_call_target="tpu_custom_call" | custom-call | tf_op jit(solution)/shard_map/panels_by_vectors/pallas_call | solution.py:262
  85.7 2.3 %copy.4 = f32[2048,128]{1,0:T(8,128)} copy(f32[2048,128]{1,0:T(8,128)} %panels_by_vectors.1) | data formatting | bytes 2097152

commit v2 on v0

v2 whole, which is shorter than its diff:
```python
import jax
import jax.numpy as jnp
from jax import lax
from jax.experimental import pallas as pl
from jax.experimental.pallas import tpu as pltpu
from jax.sharding import PartitionSpec as P

MESH = pl.DeviceIdType.MESH
CHUNKS = 8
ITEMS = 2 * CHUNKS
PIECES = 4
BK = 128
HALF = BK // 2


def remote(src, dst, send, recv, device):
    return pltpu.make_async_remote_copy(src_ref=src, dst_ref=dst, send_sem=send, recv_sem=recv, device_id=device, device_id_type=MESH)


def drain(ref, sem):
    pltpu.make_async_copy(ref, ref, sem).wait()


def parts(x):
    hi = x.astype(jnp.bfloat16)
    return hi, (x - hi.astype(jnp.float32)).astype(jnp.bfloat16)


def swap(a, b):
    left = lax.broadcasted_iota(jnp.int32, a.shape, 1) < HALF
    return jnp.where(left, a, pltpu.roll(b, HALF, 1)), jnp.where(left, pltpu.roll(a, HALF, 1), b)


def kernel(
    a_hbm, e_hbm, o_hbm,
    a_ref, e_ref, a_low, a_high, a_far, b_mine, b_first, b_second, b_far, b_all, b_cat, keep,
    go_up, go_down, in_up, in_down, late_up, late_down, end_up, end_down, z_mine, z_in, z_pair, z_other, z_sum, o_ref,
    in_sems, out_sem, as_up, as_down, ar_low, ar_high, as_far, ar_far,
    bs_first, br_first, bs_second, br_second, bs_far, br_far, bs_plane, br_plane,
    ps_up, ps_down, pr_up, pr_down, qs_up, qs_down, qr_up, qr_down,
    zs_in, zr_in, zs_pair, zr_pair, zs_out, zr_out,
):
    layer, row, col = lax.axis_index("layer"), lax.axis_index("row"), lax.axis_index("col")
    zh, core = lax.div(row, 2), lax.rem(row, 2)
    y, x = lax.div(col, 4), lax.rem(col, 4)
    ga = x + core * (y - x)
    gb = y + core * (x - y)

    def at(a, b):
        return {"col": (1 - core) * (b * 4 + a) + core * (a * 4 + b)}

    a_up, a_down = at(lax.rem(ga + 1, 4), gb), at(lax.rem(ga + 3, 4), gb)
    b_up, b_down = at(ga, lax.rem(gb + 1, 4)), at(ga, lax.rem(gb + 3, 4))
    step = 1 - 2 * core
    zh_first, zh_second = lax.rem(zh + step + 4, 4), lax.rem(zh - step + 4, 4)
    z_first, z_second = {"row": zh_first * 2 + core}, {"row": zh_second * 2 + core}
    outer = jnp.logical_or(layer == 0, layer == 3)
    inner = jnp.logical_not(outer)
    z_inner = {"layer": 1 + lax.div(layer, 2)}
    z_partner = {"layer": lax.rem(3 - layer, 4)}
    z_outer = {"layer": lax.rem(3 * layer + 1, 4)}

    load_e = pltpu.make_async_copy(e_hbm, e_ref, in_sems.at[0])
    load_a = pltpu.make_async_copy(a_hbm, a_ref, in_sems.at[1])
    load_e.start()
    load_a.start()

    barrier = pltpu.get_barrier_semaphore()

    def greet(device):
        pl.semaphore_signal(barrier, inc=1, device_id=device, device_id_type=MESH)

    for device in (z_first, z_second, a_up, a_down, b_up, b_down):
        greet(device)

    @pl.when(outer)
    def _():
        greet(z_inner)

    @pl.when(inner)
    def _():
        greet(z_partner)
        greet(z_outer)

    @pl.when(core == 0)
    def _():
        for yy in range(4):
            greet({"row": zh * 2 + 1, "col": yy * 4 + x})
        for d in range(1, 4):
            greet({"row": zh * 2, "col": lax.rem(y + d, 4) * 4 + x})

    @pl.when(core == 1)
    def _():
        for d in range(1, 4):
            greet({"row": zh * 2 + lax.div(x, 2), "col": y * 4 + lax.rem(x + d, 4)})

        @pl.when(x < 2)
        def _():
            greet({"row": zh * 2})

    load_e.wait()
    for q in range(2):
        left, right = swap(e_ref[q, :HALF, :], e_ref[q, HALF:, :])
        b_mine[0, q] = left
        b_mine[1, q] = right
    with jax.named_scope("barrier"):
        pl.semaphore_wait(barrier, 6 + (2 - outer.astype(jnp.int32)) + 3 + core + 2 - core * lax.div(x, 2))

    firsts = [remote(b_mine.at[h], b_first.at[h], bs_first.at[h], br_first.at[h], z_first) for h in range(2)]
    seconds = [remote(b_mine.at[h], b_second.at[h], bs_second.at[h], br_second.at[h], z_second) for h in range(2)]
    b_fars = [remote(b_first.at[h], b_far.at[h], bs_far.at[h], br_far.at[h], z_first) for h in range(2)]
    rows = [pl.ds(p * (a_ref.shape[0] // PIECES), a_ref.shape[0] // PIECES) for p in range(PIECES)]
    ups = [remote(a_ref.at[r], a_low.at[r], as_up.at[p], ar_low.at[p], a_up) for p, r in enumerate(rows)]
    downs = [remote(a_ref.at[r], a_high.at[r], as_down.at[p], ar_high.at[p], a_down) for p, r in enumerate(rows)]
    a_fars = [
        remote(a_high.at[r], a_far.at[r], as_far.at[p], ar_far.at[p], a_down) if p % 2
        else remote(a_low.at[r], a_far.at[r], as_far.at[p], ar_far.at[p], a_up)
        for p, r in enumerate(rows)
    ]

    def relay(p):
        (downs if p % 2 else ups)[p].wait_recv()
        a_fars[p].start()

    blocks = ((b_mine, zh), (b_first, zh_second), (b_second, zh_first), (b_far, lax.rem(zh + 2, 4)))

    def exchange(h, k, end=False):
        held, source = blocks[k]
        src, base = held.at[h], 12 * h + 3 * k
        copies = [(
            jnp.logical_and(core == 0, source == y), src, b_all.at[h, pl.ds(2 * core, 2), y],
            bs_plane.at[base], br_plane.at[4 * h + y], {"row": zh * 2, "col": source * 4 + x},
        )]
        for q in range(2):
            copies.append((
                jnp.logical_and(core == 1, x == 2 * core + q), src.at[q], b_all.at[h, source, x],
                bs_plane.at[base + 1 + q], br_plane.at[4 * h + x], {"row": zh * 2 + 1, "col": y * 4 + 2 * core + q},
            ))
        for own, src, dst, send, recv, device in copies:
            @pl.when(jnp.logical_not(own))
            def _():
                copy = remote(src, dst, send, recv, device)
                if end:
                    copy.wait_send()
                else:
                    copy.start()

            if not end:
                @pl.when(own)
                def _():
                    pltpu.make_async_copy(src, dst, recv).start()

    firsts[0].start()
    exchange(0, 0)
    load_a.wait()
    for p in range(2):
        ups[p].start()
        downs[p].start()
    with jax.named_scope("b_sent0"):
        firsts[0].wait_send()
    seconds[0].start()
    with jax.named_scope("relay0"):
        relay(0)
    ups[2].start()
    downs[2].start()
    with jax.named_scope("b_first0"):
        firsts[0].wait_recv()
    b_fars[0].start()
    firsts[1].start()
    exchange(0, 1)
    with jax.named_scope("relay1"):
        relay(1)
    with jax.named_scope("b_second0"):
        seconds[0].wait_recv()
    exchange(0, 2)
    ups[3].start()
    downs[3].start()
    with jax.named_scope("b_sent1"):
        firsts[1].wait_send()
    seconds[1].start()
    with jax.named_scope("b_far0"):
        b_fars[0].wait_recv()
    exchange(0, 3)
    with jax.named_scope("relay2"):
        relay(2)
    with jax.named_scope("b_first1"):
        firsts[1].wait_recv()
    b_fars[1].start()
    with jax.named_scope("relay3"):
        relay(3)

    def factor(h):
        for j in range(4):
            n = lax.rem(gb + j, 4)
            drain(b_all.at[h, :, n], br_plane.at[4 * h + n])
        for j in range(0, 4, 2):
            for i in range(4):
                k = lax.rem(ga + i, 4)
                both = swap(b_all[h, k, lax.rem(gb + j, 4)], b_all[h, k, lax.rem(gb + j + 1, 4)])
                for r, block in enumerate(both):
                    hi, lo = parts(block)
                    cols = pl.ds(j * HALF, BK)
                    b_cat[pl.ds(i * BK + r * HALF, HALF), cols] = hi
                    b_cat[pl.ds(512 + i * BK + r * HALF, HALF), cols] = lo
                    b_cat[pl.ds(1024 + i * BK + r * HALF, HALF), cols] = hi

    size = a_ref.shape[0] // ITEMS
    part = size // 2

    def span(m):
        return pl.ds(pl.multiple_of(m * size, size), size)

    def top(m):
        return pl.ds(pl.multiple_of(m * part, part), part)

    def multiply(t):
        m = lax.rem(t, CHUNKS)
        r = pl.ds(pl.multiple_of(m * 2 * size, 2 * size), 2 * size)
        pairs = [parts(ref[r, :]) for ref in (a_ref, a_high, a_far, a_low)]
        his, los = [p[0] for p in pairs], [p[1] for p in pairs]
        left = jnp.concatenate(his + his + los, axis=1)
        out = jnp.dot(left, b_cat[...], preferred_element_type=jnp.float32)
        mine, above = swap(out[:size, :BK], out[size:, :BK])
        far, below = swap(out[:size, BK:], out[size:, BK:])
        keep[span(t), :] = mine
        late_up[top(t), :] = above[:part]
        late_down[top(t), :] = below[part:]
        go_up[t, 0], go_up[t, 1] = far[:part], above[part:]
        go_down[t, 0], go_down[t, 1] = far[part:], below[:part]
        remote(go_up.at[t], in_up.at[t], ps_up, pr_up.at[t], b_up).start()
        remote(go_down.at[t], in_down.at[t], ps_down, pr_down.at[t], b_down).start()

    def pass_on(m):
        drain(in_up.at[m], pr_up.at[m])
        late_up[top(m), :] += in_up[m, 0]
        remote(late_up.at[top(m)], end_up.at[top(m)], qs_up, qr_up.at[m], b_up).start()
        drain(in_down.at[m], pr_down.at[m])
        late_down[top(m), :] += in_down[m, 0]
        remote(late_down.at[top(m)], end_down.at[top(m)], qs_down, qr_down.at[m], b_down).start()

    def close_layer(m):
        drain(end_up.at[top(m)], qr_up.at[m])
        drain(end_down.at[top(m)], qr_down.at[m])
        low, high = top(2 * m), top(2 * m + 1)
        z_mine[low, :] = keep[low, :] + (end_up[top(m), :] + in_down[m, 1])
        z_mine[high, :] = keep[high, :] + (in_up[m, 1] + end_down[top(m), :])

        @pl.when(outer)
        def _():
            remote(z_mine.at[span(m)], z_in.at[span(m)], zs_in, zr_in.at[m], z_inner).start()

    def pair_up(m):
        drain(z_in.at[span(m)], zr_in.at[m])
        z_pair[span(m), :] = z_mine[span(m), :] + z_in[span(m), :]
        remote(z_pair.at[span(m)], z_other.at[span(m)], zs_pair, zr_pair.at[m], z_partner).start()

    def unpack(m):
        first, second = swap(z_sum[span(m - CHUNKS), :], z_sum[span(m), :])
        o_ref[span(2 * (m - CHUNKS)), :] = first
        o_ref[span(2 * (m - CHUNKS) + 1), :] = second
        r = pl.ds(pl.multiple_of(2 * (m - CHUNKS) * size, size), 2 * size)
        pltpu.make_async_copy(o_ref.at[r], o_hbm.at[r], out_sem).start()

    def finish(m):
        drain(z_other.at[span(m)], zr_pair.at[m])
        z_sum[span(m), :] = z_pair[span(m), :] + z_other[span(m), :]
        remote(z_sum.at[span(m)], z_sum.at[span(m)], zs_out, zr_out.at[m], z_outer).start()
        pl.when(m >= CHUNKS)(lambda: unpack(m))

    with jax.named_scope("factor0"):
        factor(0)

    stages = ((multiply, 0, None), (pass_on, 2, None), (close_layer, 4, None), (pair_up, 7, inner), (finish, 10, inner))

    def body(t, carry):
        @pl.when(jnp.logical_and(lax.rem(t, CHUNKS // PIECES) == 0, t < CHUNKS))
        def _():
            p = lax.div(t, CHUNKS // PIECES)
            r = pl.ds(pl.multiple_of(p * (a_ref.shape[0] // PIECES), 8), a_ref.shape[0] // PIECES)
            drain(a_far.at[r], ar_far.at[p])

            @pl.when(lax.rem(p, 2) == 0)
            def _():
                drain(a_high.at[r], ar_high.at[p])

            @pl.when(lax.rem(p, 2) == 1)
            def _():
                drain(a_low.at[r], ar_low.at[p])

        @pl.when(t == 2)
        def _():
            exchange(1, 0)
            exchange(1, 1)
            with jax.named_scope("b_second1"):
                seconds[1].wait_recv()
            exchange(1, 2)

        @pl.when(t == 4)
        def _():
            with jax.named_scope("b_far1"):
                b_fars[1].wait_recv()
            exchange(1, 3)

        @pl.when(t == CHUNKS)
        def _():
            with jax.named_scope("factor1"):
                factor(1)

        for stage, lag, cond in stages:
            m = t - lag
            ok = jnp.logical_and(m >= 0, m < ITEMS)
            if cond is not None:
                ok = jnp.logical_and(ok, cond)
            pl.when(ok)(lambda stage=stage, m=m: jax.named_scope(stage.__name__)(stage)(m))
        return carry

    lax.fori_loop(0, ITEMS + stages[-1][1], body, 0)

    with jax.named_scope("outs"):
        @pl.when(outer)
        def _():
            def take(m, carry):
                drain(z_sum.at[span(m)], zr_out.at[m])
                pl.when(m >= CHUNKS)(lambda: unpack(m))
                return carry

            lax.fori_loop(0, ITEMS, take, 0)
            drain(z_mine, zs_in)

        @pl.when(inner)
        def _():
            drain(z_pair, zs_pair)
            drain(z_sum, zs_out)

    with jax.named_scope("sends"):
        pltpu.make_async_copy(o_ref, o_hbm, out_sem).wait()
        for ref, sem in ((go_up, ps_up), (go_down, ps_down), (late_up, qs_up), (late_down, qs_down)):
            drain(ref, sem)
        for c in seconds + b_fars + ups + downs + a_fars:
            c.wait_send()
        for h in range(2):
            for k in range(4):
                exchange(h, k, end=True)


def local(panels, eigvecs):
    m, f32 = panels.shape[0], jnp.float32
    whole = pltpu.VMEM((m, BK), f32)
    block = pltpu.VMEM((2, 2, HALF, BK), f32)
    dma = pltpu.SemaphoreType.DMA
    both = pltpu.VMEM((ITEMS, 2, m // ITEMS // 2, BK), f32)
    late = pltpu.VMEM((m // 2, BK), f32)
    pieces, items = dma((PIECES,)), dma((ITEMS,))
    return pl.pallas_call(
        kernel,
        out_shape=jax.ShapeDtypeStruct((m, BK), f32),
        in_specs=[pl.BlockSpec(memory_space=pltpu.HBM)] * 2,
        out_specs=pl.BlockSpec(memory_space=pl.ANY),
        scratch_shapes=[
            whole, pltpu.VMEM((2, BK, BK), f32), whole, whole, whole, block, block, block, block,
            pltpu.VMEM((2, 4, 4, HALF, BK), f32), pltpu.VMEM((12 * BK, 2 * BK), jnp.bfloat16), whole,
            both, both, both, both, late, late, late, late, whole, whole, whole, whole, whole, whole,
            dma((2,)), dma, pieces, pieces, pieces, pieces, pieces, pieces,
            dma((2,)), dma((2,)), dma((2,)), dma((2,)), dma((2,)), dma((2,)), dma((24,)), dma((8,)),
            dma, dma, items, items, dma, dma, items, items,
            dma, items, dma, items, dma, items,
        ],
        compiler_params=pltpu.CompilerParams(collective_id=0, has_side_effects=True, vmem_limit_bytes=53 * 2**20),
        name="panels_by_vectors",
    )(panels, eigvecs.reshape(2, BK, BK))


def solution(mesh):
    in_specs = (P("row", ("layer", "col")), P(("layer", "row"), "col"))
    return jax.shard_map(local, mesh=mesh, in_specs=in_specs, out_specs=P("row", "col"), check_vma=False)
```

time: 230 us -> 83.8 us (0.36)
  blocking collectives: 122 us -> 0 us
  Pallas kernels: 0 us -> 80.3 us
  waiting for transfers between devices: 76 us -> 0 us
  matrix products: 15.9 us -> 0 us
  between operations: 13.4 us -> 0.01 us
    all_to_all x3 -> x0, blocking collectives: 122 us -> none  [the longest x2 93 us: from_everyone(): lax.all_to_all(jnp.broadcast_to(x[None], (devices, *x.shape)), axis, 0, 0...]
    pallas_call x0 -> x1, Pallas kernels: none -> 80.3 us  [local(): pl.pallas_call(kernel, out_shape=jax.ShapeDtypeStruct((m, BK), f32), in_s...]
    all_gather x1 -> x0, waiting for transfers between devices: 75.3 us -> none  [local(): lax.all_gather(panels, 'col', axis=1, tiled=True)]
    dot_general x1 -> x0, matrix products: 15.9 us -> none  [local(): jnp.dot(lax.all_gather(panels, 'col', axis=1, tiled=True), layer_vecs, pr...]
  transfers between devices with their start and end apart: 1 -> 0, of which waited for: 1 -> 0; matrix products, arithmetic and copies ran while one was open for 0% -> 0% of each run, Pallas kernels for 0% -> 0%
where the time goes in v2:
time: 83.8 us; the launch traced here: 83.5 us
  Pallas kernels  80.3 us (96%)
  local copies, waits for them, and re-layouts  3.17 us (4%)
    pallas_call x1, Pallas kernels, local(): pl.pallas_call(kernel, out_shape=jax.ShapeDtypeStruct((m, BK), f32), in_s...  80.3 us
    unnamed x3, local copies, waits for them, and re-layouts  3.17 us

profile of v2, /device:TPU:24, one launch (start us, length us, event | category | flops | bytes accessed | tf_op | source)
XLA Modules:
  0.0 83.5 jit_solution(15432711422405992850)
XLA Ops:
  0.0 0.0 copy-start
  0.0 0.9 %copy-done = f32[256,128]{1,0:T(8,128)S(1)} copy-done((f32[256,128]{1,0:T(8,128)S(1)}, f32[256,128]{1,0:T(8,128)}, u32[]{:S(2)}) %copy-start) | copy-done | bytes 131096
  0.9 80.3 %panels_by_vectors.1 = f32[2048,128]{1,0:T(8,128)} custom-call(f32[2048,128]{1,0:T(8,128)} %a_hbm.1, f32[2,128,128]{2,1,0:T(8,128)S(1)} %bitcast.1), custom_call_target="tpu_custom_call" | custom-call | tf_op jit(solution)/shard_map/panels_by_vectors/pallas_call | solution.py:354
  81.2 2.3 %copy.4 = f32[2048,128]{1,0:T(8,128)} copy(f32[2048,128]{1,0:T(8,128)} %panels_by_vectors.1) | data formatting | bytes 2097152
Async XLA Ops:
  0.0 0.9 %copy-start = (f32[256,128]{1,0:T(8,128)S(1)}, f32[256,128]{1,0:T(8,128)}, u32[]{:S(2)}) copy-start(f32[256,128]{1,0:T(8,128)} %param.3) | copy-start | bytes 393220

commit v3 on v0

v3 whole, which is shorter than its diff:
```python
import jax
import jax.numpy as jnp
from jax import lax
from jax.experimental import pallas as pl
from jax.experimental.pallas import tpu as pltpu
from jax.sharding import PartitionSpec as P

MESH = pl.DeviceIdType.MESH
BK = 128
QUARTERS = 4
QUARTER = BK // QUARTERS
PIECES = 4
ITEMS = QUARTERS * PIECES
LAGS = (2, 5, 8, 11)


def remote(src, dst, send, recv, device):
    return pltpu.make_async_remote_copy(src_ref=src, dst_ref=dst, send_sem=send, recv_sem=recv, device_id=device, device_id_type=MESH)


def drain(ref, sem):
    pltpu.make_async_copy(ref, ref, sem).wait()


def parts(x):
    hi = x.astype(jnp.bfloat16)
    return hi, (x - hi.astype(jnp.float32)).astype(jnp.bfloat16)


def swap(a, b, width):
    even = lax.rem(lax.div(lax.broadcasted_iota(jnp.int32, a.shape, 1), width), 2) == 0
    return jnp.where(even, a, pltpu.roll(b, width, 1)), jnp.where(even, pltpu.roll(a, BK - width, 1), b)


def turn(x):
    a, b = swap(x[0], x[2], 2 * QUARTER)
    c, d = swap(x[1], x[3], 2 * QUARTER)
    return (*swap(a, c, QUARTER), *swap(b, d, QUARTER))


def kernel(
    a_hbm, e_hbm, o_hbm,
    a_ref, e_ref, o_ref, a_low, a_high, a_far, a_cat, b_mine, b_first, b_second, b_far, b_all, b_cat, keep,
    go_up, go_down, in_up, in_down, late_up, late_down, end_up, end_down, z_mine, z_in, z_pair, z_other, z_sum,
    in_sems, out_sem, plane_sem, z_sem, as_near, as_far, ar_low, ar_high, ar_far,
    bs_lead, bs_first, bs_second, bs_far, br_first, br_second, br_far, bs_plane, br_plane,
    ps_up, ps_down, pr, qs_up, qs_down, qr, zs_in, zr_in, zs_pair, zr_pair, zs_out, zr_out,
):
    layer, row, col = lax.axis_index("layer"), lax.axis_index("row"), lax.axis_index("col")
    zh, core = lax.div(row, 2), lax.rem(row, 2)
    y, x = lax.div(col, 4), lax.rem(col, 4)
    ga = x + core * (y - x)
    gb = y + core * (x - y)

    def at(a, b):
        return {"col": (1 - core) * (b * 4 + a) + core * (a * 4 + b)}

    a_up, a_down = at(lax.rem(ga + 1, 4), gb), at(lax.rem(ga + 3, 4), gb)
    b_up, b_down = at(ga, lax.rem(gb + 1, 4)), at(ga, lax.rem(gb + 3, 4))
    step = 1 - 2 * core
    zh_first, zh_second = lax.rem(zh + step + 4, 4), lax.rem(zh - step + 4, 4)
    z_first, z_second = {"row": zh_first * 2 + core}, {"row": zh_second * 2 + core}
    outer = jnp.logical_or(layer == 0, layer == 3)
    inner = jnp.logical_not(outer)
    z_inner = 1 + lax.div(layer, 2)
    z_partner = lax.rem(3 - layer, 4)
    z_outer = lax.rem(3 * layer + 1, 4)
    early = zh < 2
    lead = early.astype(jnp.int32)

    load_e = pltpu.make_async_copy(e_hbm, e_ref, in_sems.at[0])
    load_a = pltpu.make_async_copy(a_hbm, a_ref, in_sems.at[1])
    load_e.start()
    load_a.start()

    barrier = pltpu.get_barrier_semaphore()

    def greet(device):
        pl.semaphore_signal(barrier, inc=1, device_id=device, device_id_type=MESH)

    core0, core1 = zh * 2, zh * 2 + 1
    for d in (1, 3):
        greet({"row": lax.rem(zh + d, 4) * 2})

    @pl.when(outer)
    def _():
        greet({"row": core0, "layer": z_inner})

    @pl.when(inner)
    def _():
        greet({"row": core0, "layer": z_partner})
        greet({"row": core0, "layer": z_outer})

    for d in (1, 3, 2):
        greet({"row": core1, "col": y * 4 + lax.rem(x + d, 4)})
        greet({"row": core1, "col": lax.rem(y + d, 4) * 4 + x})

    @pl.when(core == 0)
    def _():
        greet({"row": core1})

    @pl.when(core == 1)
    def _():
        greet({"row": core0})

    load_e.wait()
    for h in range(2):
        for q, packed in enumerate(turn([e_ref[h, pl.ds(g * QUARTER, QUARTER), :] for g in range(4)])):
            b_mine[q, h] = packed

    with jax.named_scope("plane_barrier"):
        @pl.when(core == 1)
        def _():
            pl.semaphore_wait(barrier, 13)
            pl.semaphore_signal(plane_sem, inc=1, device_id={"row": core0}, device_id_type=MESH)

        @pl.when(core == 0)
        def _():
            pl.semaphore_wait(plane_sem, 1)

    rows = [pl.ds(p * (a_ref.shape[0] // PIECES), a_ref.shape[0] // PIECES) for p in range(PIECES)]
    ups = [remote(a_ref.at[r], a_low.at[r], as_near, ar_low.at[p], a_up) for p, r in enumerate(rows)]
    downs = [remote(a_ref.at[r], a_high.at[r], as_near, ar_high.at[p], a_down) for p, r in enumerate(rows)]
    a_fars = [
        remote(a_high.at[r], a_far.at[r], as_far, ar_far.at[p], a_down) if p % 2
        else remote(a_low.at[r], a_far.at[r], as_far, ar_far.at[p], a_up)
        for p, r in enumerate(rows)
    ]

    def send_piece(p):
        ups[p].start()
        downs[p].start()

    def relay(p):
        with jax.named_scope(f"relay{p}"):
            (downs if p % 2 else ups)[p].wait_recv()
        a_fars[p].start()

    firsts = [remote(b_mine.at[q], b_first.at[q], bs_first if q else bs_lead, br_first.at[q], z_first) for q in range(QUARTERS)]
    seconds = [remote(b_mine.at[q], b_second.at[q], bs_second, br_second.at[q], z_second) for q in range(QUARTERS)]
    b_fars = [remote(b_first.at[q], b_far.at[q], bs_far, br_far.at[q], z_first) for q in range(QUARTERS)]
    blocks = ((b_mine, zh), (b_first, zh_second), (b_second, zh_first), (b_far, lax.rem(zh + 2, 4)))

    def exchange(q, k):
        held, source = blocks[k]
        src = held.at[q]
        copies = [(jnp.logical_and(core == 0, source == y), src, b_all.at[q, pl.ds(2 * core, 2), y], {"row": core0, "col": source * 4 + x})]
        for h in range(2):
            copies.append((
                jnp.logical_and(core == 1, x == 2 * core + h), src.at[h], b_all.at[q, source, x], {"row": core1, "col": y * 4 + 2 * core + h},
            ))
        for own, src, dst, device in copies:
            @pl.when(own)
            def _():
                pltpu.make_async_copy(src, dst, br_plane.at[q]).start()

            @pl.when(jnp.logical_not(own))
            def _():
                remote(src, dst, bs_plane, br_plane.at[q], device).start()

    def arrived(copies, q):
        name = "b_first" if copies is firsts else "b_second" if copies is seconds else "b_far"
        with jax.named_scope(f"{name}{q}"):
            copies[q].wait_recv()

    exchange(0, 0)
    load_a.wait()
    send_piece(0)
    send_piece(1)

    @pl.when(early)
    def _():
        send_piece(2)
        send_piece(3)

    @pl.when(zh == 0)
    def _():
        relay(0)

    with jax.named_scope("z_barrier"):
        @pl.when(core == 0)
        def _():
            pl.semaphore_wait(barrier, 7 + 2 * inner.astype(jnp.int32))
            pl.semaphore_signal(z_sem, inc=1, device_id={"row": core1}, device_id_type=MESH)

        @pl.when(core == 1)
        def _():
            pl.semaphore_wait(z_sem, 1)

    firsts[0].start()
    with jax.named_scope("b_lead"):
        firsts[0].wait_send()
    seconds[0].start()
    firsts[1].start()
    arrived(firsts, 0)
    b_fars[0].start()
    firsts[2].start()
    exchange(0, 1)
    pl.when(zh != 0)(lambda: relay(0))
    pl.when(zh == 0)(lambda: relay(1))
    arrived(seconds, 0)
    exchange(0, 2)
    seconds[1].start()
    arrived(firsts, 1)
    b_fars[1].start()
    pl.when(zh != 0)(lambda: relay(1))
    pl.when(early)(lambda: relay(2))
    pl.when(jnp.logical_not(early))(lambda: send_piece(2))
    arrived(b_fars, 0)
    exchange(0, 3)
    firsts[3].start()
    exchange(1, 0)
    exchange(1, 1)
    arrived(firsts, 2)
    b_fars[2].start()
    seconds[2].start()
    pl.when(early)(lambda: relay(3))

    @pl.when(jnp.logical_not(early))
    def _():
        relay(2)
        send_piece(3)

    arrived(seconds, 1)
    exchange(1, 2)

    def factor(q):
        with jax.named_scope(f"factor{q}"):
            drain(b_all.at[q], br_plane.at[q])
            for i in range(4):
                k = lax.rem(ga + i, 4)
                for g, block in enumerate(turn([b_all[q, k, lax.rem(gb + j, 4)] for j in range(4)])):
                    hi, lo = parts(block)
                    for r in (i * BK + g * QUARTER, 4 * BK + i * BK + g * QUARTER):
                        b_cat[q, pl.ds(r, QUARTER), pl.ds(0, BK)] = hi
                        b_cat[q, pl.ds(r, QUARTER), pl.ds(BK, BK)] = lo

    size = a_ref.shape[0] // ITEMS
    part = size // 2

    def span(m):
        return pl.ds(pl.multiple_of(m * size, size), size)

    def top(m):
        return pl.ds(pl.multiple_of(m * part, part), part)

    def place(t):
        b, c = lax.div(t, 9), lax.div(t, 12)
        q = (1 - b) * lax.div(t, 3) + (b - c) * (t - 9) + c * 3
        p = (1 - b) * lax.rem(t, 3) + (b - c) * 3 + c * (t - 12)
        return lead * lax.div(t, PIECES) + (1 - lead) * q, lead * lax.rem(t, PIECES) + (1 - lead) * p

    def item(q, p):
        b = lax.div(p, 3)
        return lead * (PIECES * q + p) + (1 - lead) * ((1 - b) * (3 * q + p) + b * (9 + q))

    def whole(p):
        return pl.ds(pl.multiple_of(p * 4 * size, 4 * size), 4 * size)

    def take_piece(p):
        r = whole(p)
        with jax.named_scope("piece"):
            drain(a_far.at[r], ar_far.at[p])

            @pl.when(lax.rem(p, 2) == 0)
            def _():
                drain(a_high.at[r], ar_high.at[p])

            @pl.when(lax.rem(p, 2) == 1)
            def _():
                drain(a_low.at[r], ar_low.at[p])

        for i, ref in enumerate((a_ref, a_high, a_far, a_low)):
            hi, lo = parts(ref[r, :])
            a_cat[r, pl.ds(i * BK, BK)] = hi
            a_cat[r, pl.ds((4 + i) * BK, BK)] = lo

    def multiply(t):
        q, p = place(t)
        pl.when(q == 0)(lambda: take_piece(p))
        out = jnp.dot(a_cat[whole(p), :], b_cat[q], preferred_element_type=jnp.float32)
        out = out[:, :BK] + out[:, BK:]
        mine, above, far, below = turn([out[g * size:(g + 1) * size] for g in range(4)])
        keep[span(t), :] = mine
        late_up[top(t), :] = above[:part]
        late_down[top(t), :] = below[part:]
        go_up[t, 0], go_up[t, 1] = far[:part], above[part:]
        go_down[t, 0], go_down[t, 1] = far[part:], below[:part]
        remote(go_up.at[t], in_up.at[t], ps_up, pr.at[t, 0], b_up).start()
        remote(go_down.at[t], in_down.at[t], ps_down, pr.at[t, 1], b_down).start()

    def pass_on(m):
        drain(in_up.at[m], pr.at[m, 0])
        late_up[top(m), :] += in_up[m, 0]
        remote(late_up.at[top(m)], end_up.at[top(m)], qs_up, qr.at[m], b_up).start()
        drain(in_down.at[m], pr.at[m, 1])
        late_down[top(m), :] += in_down[m, 0]
        remote(late_down.at[top(m)], end_down.at[top(m)], qs_down, qr.at[m], b_down).start()

    def close_layer(m):
        drain(z_mine.at[span(m)], qr.at[m])
        low, high = top(2 * m), top(2 * m + 1)
        z_mine[low, :] = keep[low, :] + (end_up[top(m), :] + in_down[m, 1])
        z_mine[high, :] = keep[high, :] + (in_up[m, 1] + end_down[top(m), :])

        @pl.when(outer)
        def _():
            remote(z_mine.at[span(m)], z_in.at[span(m)], zs_in, zr_in.at[m], {"layer": z_inner}).start()

    def pair_up(m):
        drain(z_in.at[span(m)], zr_in.at[m])
        z_pair[span(m), :] = z_mine[span(m), :] + z_in[span(m), :]
        remote(z_pair.at[span(m)], z_other.at[span(m)], zs_pair, zr_pair.at[m], {"layer": z_partner}).start()

    def unpack(t):
        q, p = place(t)

        @pl.when(q == 3)
        def _():
            for g, block in enumerate(turn([z_sum[span(m), :] for m in [item(i, p) for i in range(QUARTERS - 1)] + [t]])):
                o_ref[span(4 * p + g), :] = block
            pltpu.make_async_copy(o_ref.at[whole(p)], o_hbm.at[whole(p)], out_sem).start()

    def finish(m):
        drain(z_other.at[span(m)], zr_pair.at[m])
        z_sum[span(m), :] = z_pair[span(m), :] + z_other[span(m), :]
        remote(z_sum.at[span(m)], z_sum.at[span(m)], zs_out, zr_out.at[m], {"layer": z_outer}).start()
        unpack(m)

    def run(stage, m):
        jax.named_scope(stage.__name__)(stage)(m)

    factor(0)
    run(multiply, 0)
    arrived(b_fars, 1)
    exchange(1, 3)
    run(multiply, 1)
    exchange(2, 0)
    exchange(2, 1)
    arrived(seconds, 2)
    exchange(2, 2)
    arrived(firsts, 3)
    b_fars[3].start()
    seconds[3].start()
    pl.when(jnp.logical_not(early))(lambda: run(pass_on, 0))
    run(multiply, 2)
    pl.when(early)(lambda: run(pass_on, 0))
    pl.when(jnp.logical_not(early))(lambda: relay(3))
    arrived(b_fars, 2)
    exchange(2, 3)
    pl.when(jnp.logical_not(early))(lambda: factor(1))
    run(multiply, 3)
    run(pass_on, 1)
    stages = tuple(zip((multiply, pass_on, close_layer, pair_up, finish), (0, *LAGS), (4, 2, 0, 0, 0), (None, None, None, inner, inner)))

    def body(t, carry):
        pl.when(jnp.logical_and(early, t == 4))(lambda: factor(1))
        pl.when(t == 6 + 2 * lead)(lambda: factor(2))

        @pl.when(t == 5)
        def _():
            exchange(3, 0)
            exchange(3, 1)

        @pl.when(t == 6)
        def _():
            arrived(seconds, 3)
            exchange(3, 2)

        @pl.when(t == 7)
        def _():
            arrived(b_fars, 3)
            exchange(3, 3)

        pl.when(t == 12)(lambda: factor(3))
        for stage, lag, least, cond in stages:
            m = t - lag
            ok = jnp.logical_and(m >= least, m < ITEMS)
            if cond is not None:
                ok = jnp.logical_and(ok, cond)
            pl.when(ok)(lambda stage=stage, m=m: run(stage, m))
        return carry

    lax.fori_loop(4, ITEMS + LAGS[-1], body, 0)

    with jax.named_scope("outs"):
        @pl.when(outer)
        def _():
            def take(m, carry):
                drain(z_sum.at[span(m)], zr_out.at[m])
                unpack(m)
                return carry

            lax.fori_loop(0, ITEMS, take, 0)
            drain(z_mine, zs_in)

        @pl.when(inner)
        def _():
            drain(z_pair, zs_pair)
            drain(z_sum, zs_out)

    with jax.named_scope("sends"):
        for ref, sem in ((go_up, ps_up), (go_down, ps_down), (late_up, qs_up), (late_down, qs_down)):
            drain(ref, sem)
        drain(a_ref, as_near)
        drain(a_ref, as_near)
        drain(a_far, as_far)
        drain(b_mine.at[pl.ds(1, 3)], bs_first)
        drain(b_mine, bs_second)
        drain(b_first, bs_far)
        for own, sent in ((core == 0, 14), (jnp.logical_and(core == 1, x < 2), 16), (jnp.logical_and(core == 1, x >= 2), 12)):
            pl.when(own)(lambda sent=sent: drain(a_ref.at[pl.ds(0, sent * BK)], bs_plane))
        pltpu.make_async_copy(o_ref, o_hbm, out_sem).wait()


def local(panels, eigvecs):
    m, f32, bf16 = panels.shape[0], jnp.float32, jnp.bfloat16
    whole = pltpu.VMEM((m, BK), f32)
    block = pltpu.VMEM((QUARTERS, 2, QUARTER, BK), f32)
    both = pltpu.VMEM((ITEMS, 2, m // ITEMS // 2, BK), f32)
    late = pltpu.VMEM((m // 2, BK), f32)
    dma, regular = pltpu.SemaphoreType.DMA, pltpu.SemaphoreType.REGULAR
    four, items = dma((4,)), dma((ITEMS,))
    return pl.pallas_call(
        kernel,
        out_shape=jax.ShapeDtypeStruct((m, BK), f32),
        in_specs=[pl.BlockSpec(memory_space=pltpu.HBM)] * 2,
        out_specs=pl.BlockSpec(memory_space=pl.ANY),
        scratch_shapes=[
            whole, pltpu.VMEM((2, BK, BK), f32), whole, whole, whole, whole, pltpu.VMEM((m, 8 * BK), bf16), block, block, block, block,
            pltpu.VMEM((QUARTERS, 4, 4, QUARTER, BK), f32), pltpu.VMEM((QUARTERS, 8 * BK, 2 * BK), bf16), whole,
            both, both, both, both, late, late, late, late, whole, whole, whole, whole, whole,
            dma((2,)), dma, regular, regular, dma, dma, four, four, four,
            dma, dma, dma, dma, four, four, four, dma, four,
            dma, dma, dma((ITEMS, 2)), dma, dma, items, dma, items, dma, items, dma, items,
        ],
        compiler_params=pltpu.CompilerParams(collective_id=0, has_side_effects=True, vmem_limit_bytes=52 * 2**20),
        name="panels_by_vectors",
    )(panels, eigvecs.reshape(2, BK, BK))


def solution(mesh):
    in_specs = (P("row", ("layer", "col")), P(("layer", "row"), "col"))
    return jax.shard_map(local, mesh=mesh, in_specs=in_specs, out_specs=P("row", "col"), check_vma=False)
```

time: 230 us -> 76.4 us (0.33)
  blocking collectives: 122 us -> 0 us
  waiting for transfers between devices: 76 us -> 0 us
  Pallas kernels: 0 us -> 74.2 us
  matrix products: 15.9 us -> 0 us
  between operations: 13.4 us -> 0.01 us
    all_to_all x3 -> x0, blocking collectives: 122 us -> none  [the longest x2 93 us: from_everyone(): lax.all_to_all(jnp.broadcast_to(x[None], (devices, *x.shape)), axis, 0, 0...]
    all_gather x1 -> x0, waiting for transfers between devices: 75.3 us -> none  [local(): lax.all_gather(panels, 'col', axis=1, tiled=True)]
    pallas_call x0 -> x1, Pallas kernels: none -> 74.2 us  [local(): pl.pallas_call(kernel, out_shape=jax.ShapeDtypeStruct((m, BK), f32), in_s...]
    dot_general x1 -> x0, matrix products: 15.9 us -> none  [local(): jnp.dot(lax.all_gather(panels, 'col', axis=1, tiled=True), layer_vecs, pr...]
  transfers between devices with their start and end apart: 1 -> 0, of which waited for: 1 -> 0; matrix products, arithmetic and copies ran while one was open for 0% -> 0% of each run, Pallas kernels for 0% -> 0%
where the time goes in v3:
time: 76.4 us; the launch traced here: 76.1 us
  Pallas kernels  74.2 us (97%)
  local copies, waits for them, and re-layouts  1.88 us (2%)
    pallas_call x1, Pallas kernels, local(): pl.pallas_call(kernel, out_shape=jax.ShapeDtypeStruct((m, BK), f32), in_s...  74.2 us
    unnamed x3, local copies, waits for them, and re-layouts  1.88 us

profile of v3, /device:TPU:24, one launch (start us, length us, event | category | flops | bytes accessed | tf_op | source)
XLA Modules:
  0.0 76.1 jit_solution(15802002030397393366)
XLA Ops:
  0.0 0.0 copy-start
  0.0 0.9 %copy-done = f32[256,128]{1,0:T(8,128)S(1)} copy-done((f32[256,128]{1,0:T(8,128)S(1)}, f32[256,128]{1,0:T(8,128)}, u32[]{:S(2)}) %copy-start) | copy-done | bytes 131096
  0.9 74.2 %panels_by_vectors.1 = f32[2048,128]{1,0:T(8,128)S(1)} custom-call(f32[2048,128]{1,0:T(8,128)} %a_hbm.1, f32[2,128,128]{2,1,0:T(8,128)S(1)} %bitcast.1), custom_call_target="tpu_custom_call" | custom-call | tf_op jit(solution)/shard_map/panels_by_vectors/pallas_call | solution.py:424
  75.1 1.0 %copy.4 = f32[2048,128]{1,0:T(8,128)} copy(f32[2048,128]{1,0:T(8,128)S(1)} %panels_by_vectors.1) | data formatting | bytes 2097152
Async XLA Ops:
  0.0 0.9 %copy-start = (f32[256,128]{1,0:T(8,128)S(1)}, f32[256,128]{1,0:T(8,128)}, u32[]{:S(2)}) copy-start(f32[256,128]{1,0:T(8,128)} %param.3) | copy-start | bytes 393220

commit v4 on v3

--- a/solution.py
+++ b/solution.py
@@ -11,7 +11,9 @@
 QUARTER = BK // QUARTERS
 PIECES = 4
 ITEMS = QUARTERS * PIECES
-LAGS = (2, 5, 8, 11)
+SPLIT = 4
+LAGS = (3, 6, 8, 11)
+SLOWER = {"pass_on": (8,), "close_layer": (8, 10)}
 
 
 def remote(src, dst, send, recv, device):
@@ -79,17 +81,21 @@
         pl.semaphore_signal(barrier, inc=1, device_id=device, device_id_type=MESH)
 
     core0, core1 = zh * 2, zh * 2 + 1
+    def greet_z(there, layers):
+        greet({"row": there * 2, **layers})
+        pl.when(there >= 2)(lambda: greet({"row": there * 2 + 1, **layers}))
+
     for d in (1, 3):
-        greet({"row": lax.rem(zh + d, 4) * 2})
+        greet_z(lax.rem(zh + d, 4), {})
 
     @pl.when(outer)
     def _():
-        greet({"row": core0, "layer": z_inner})
+        greet_z(zh, {"layer": z_inner})
 
     @pl.when(inner)
     def _():
-        greet({"row": core0, "layer": z_partner})
-        greet({"row": core0, "layer": z_outer})
+        greet_z(zh, {"layer": z_partner})
+        greet_z(zh, {"layer": z_outer})
 
     for d in (1, 3, 2):
         greet({"row": core1, "col": y * 4 + lax.rem(x + d, 4)})
@@ -111,7 +117,7 @@
     with jax.named_scope("plane_barrier"):
         @pl.when(core == 1)
         def _():
-            pl.semaphore_wait(barrier, 13)
+            pl.semaphore_wait(barrier, 13 + (1 - lead) * (6 + 2 * inner.astype(jnp.int32)))
             pl.semaphore_signal(plane_sem, inc=1, device_id={"row": core0}, device_id_type=MESH)
 
         @pl.when(core == 0)
@@ -163,27 +169,54 @@
         with jax.named_scope(f"{name}{q}"):
             copies[q].wait_recv()
 
+    size = a_ref.shape[0] // ITEMS
+    part = size // 2
+
+    def span(m):
+        return pl.ds(pl.multiple_of(m * size, size), size)
+
+    def top(m):
+        return pl.ds(pl.multiple_of(m * part, part), part)
+
+    def whole(p):
+        return pl.ds(pl.multiple_of(p * 4 * size, 4 * size), 4 * size)
+
+    def take_piece(p):
+        r = whole(p)
+        with jax.named_scope("piece"):
+            drain(a_far.at[r], ar_far.at[p])
+
+            @pl.when(lax.rem(p, 2) == 0)
+            def _():
+                drain(a_high.at[r], ar_high.at[p])
+
+            @pl.when(lax.rem(p, 2) == 1)
+            def _():
+                drain(a_low.at[r], ar_low.at[p])
+
+        for i, ref in enumerate((a_ref, a_high, a_far, a_low)):
+            hi, lo = parts(ref[r, :])
+            a_cat[r, pl.ds(i * BK, BK)] = hi
+            a_cat[r, pl.ds((4 + i) * BK, BK)] = lo
+
     exchange(0, 0)
     load_a.wait()
     send_piece(0)
     send_piece(1)
 
-    @pl.when(early)
+    @pl.when(zh == 0)
     def _():
         send_piece(2)
         send_piece(3)
-
-    @pl.when(zh == 0)
-    def _():
         relay(0)
 
     with jax.named_scope("z_barrier"):
         @pl.when(core == 0)
         def _():
             pl.semaphore_wait(barrier, 7 + 2 * inner.astype(jnp.int32))
-            pl.semaphore_signal(z_sem, inc=1, device_id={"row": core1}, device_id_type=MESH)
-
-        @pl.when(core == 1)
+            pl.when(early)(lambda: pl.semaphore_signal(z_sem, inc=1, device_id={"row": core1}, device_id_type=MESH))
+
+        @pl.when(jnp.logical_and(core == 1, early))
         def _():
             pl.semaphore_wait(z_sem, 1)
 
@@ -192,25 +225,37 @@
         firsts[0].wait_send()
     seconds[0].start()
     firsts[1].start()
+
+    @pl.when(zh == 1)
+    def _():
+        relay(0)
+        send_piece(2)
+
     arrived(firsts, 0)
     b_fars[0].start()
     firsts[2].start()
     exchange(0, 1)
-    pl.when(zh != 0)(lambda: relay(0))
-    pl.when(zh == 0)(lambda: relay(1))
+    pl.when(jnp.logical_not(early))(lambda: relay(0))
+    pl.when(early)(lambda: relay(1))
+    pl.when(zh == 1)(lambda: send_piece(3))
     arrived(seconds, 0)
     exchange(0, 2)
     seconds[1].start()
     arrived(firsts, 1)
     b_fars[1].start()
-    pl.when(zh != 0)(lambda: relay(1))
     pl.when(early)(lambda: relay(2))
-    pl.when(jnp.logical_not(early))(lambda: send_piece(2))
+
+    @pl.when(jnp.logical_not(early))
+    def _():
+        relay(1)
+        send_piece(2)
+
     arrived(b_fars, 0)
     exchange(0, 3)
     firsts[3].start()
     exchange(1, 0)
     exchange(1, 1)
+    take_piece(0)
     arrived(firsts, 2)
     b_fars[2].start()
     seconds[2].start()
@@ -223,6 +268,9 @@
 
     arrived(seconds, 1)
     exchange(1, 2)
+    take_piece(1)
+    arrived(b_fars, 1)
+    exchange(1, 3)
 
     def factor(q):
         with jax.named_scope(f"factor{q}"):
@@ -235,15 +283,6 @@
                         b_cat[q, pl.ds(r, QUARTER), pl.ds(0, BK)] = hi
                         b_cat[q, pl.ds(r, QUARTER), pl.ds(BK, BK)] = lo
 
-    size = a_ref.shape[0] // ITEMS
-    part = size // 2
-
-    def span(m):
-        return pl.ds(pl.multiple_of(m * size, size), size)
-
-    def top(m):
-        return pl.ds(pl.multiple_of(m * part, part), part)
-
     def place(t):
         b, c = lax.div(t, 9), lax.div(t, 12)
         q = (1 - b) * lax.div(t, 3) + (b - c) * (t - 9) + c * 3
@@ -254,30 +293,9 @@
         b = lax.div(p, 3)
         return lead * (PIECES * q + p) + (1 - lead) * ((1 - b) * (3 * q + p) + b * (9 + q))
 
-    def whole(p):
-        return pl.ds(pl.multiple_of(p * 4 * size, 4 * size), 4 * size)
-
-    def take_piece(p):
-        r = whole(p)
-        with jax.named_scope("piece"):
-            drain(a_far.at[r], ar_far.at[p])
-
-            @pl.when(lax.rem(p, 2) == 0)
-            def _():
-                drain(a_high.at[r], ar_high.at[p])
-
-            @pl.when(lax.rem(p, 2) == 1)
-            def _():
-                drain(a_low.at[r], ar_low.at[p])
-
-        for i, ref in enumerate((a_ref, a_high, a_far, a_low)):
-            hi, lo = parts(ref[r, :])
-            a_cat[r, pl.ds(i * BK, BK)] = hi
-            a_cat[r, pl.ds((4 + i) * BK, BK)] = lo
-
     def multiply(t):
         q, p = place(t)
-        pl.when(q == 0)(lambda: take_piece(p))
+        pl.when(jnp.logical_and(q == 0, p >= 2))(lambda: take_piece(p))
         out = jnp.dot(a_cat[whole(p), :], b_cat[q], preferred_element_type=jnp.float32)
         out = out[:, :BK] + out[:, BK:]
         mine, above, far, below = turn([out[g * size:(g + 1) * size] for g in range(4)])
@@ -286,14 +304,13 @@
         late_down[top(t), :] = below[part:]
         go_up[t, 0], go_up[t, 1] = far[:part], above[part:]
         go_down[t, 0], go_down[t, 1] = far[part:], below[:part]
-        remote(go_up.at[t], in_up.at[t], ps_up, pr.at[t, 0], b_up).start()
-        remote(go_down.at[t], in_down.at[t], ps_down, pr.at[t, 1], b_down).start()
+        remote(go_up.at[t], in_up.at[t], ps_up, pr.at[t], b_up).start()
+        remote(go_down.at[t], in_down.at[t], ps_down, pr.at[t], b_down).start()
 
     def pass_on(m):
-        drain(in_up.at[m], pr.at[m, 0])
+        drain(a_ref.at[pl.ds(0, 2 * size)], pr.at[m])
         late_up[top(m), :] += in_up[m, 0]
         remote(late_up.at[top(m)], end_up.at[top(m)], qs_up, qr.at[m], b_up).start()
-        drain(in_down.at[m], pr.at[m, 1])
         late_down[top(m), :] += in_down[m, 0]
         remote(late_down.at[top(m)], end_down.at[top(m)], qs_down, qr.at[m], b_down).start()
 
@@ -303,14 +320,26 @@
         z_mine[low, :] = keep[low, :] + (end_up[top(m), :] + in_down[m, 1])
         z_mine[high, :] = keep[high, :] + (in_up[m, 1] + end_down[top(m), :])
 
-        @pl.when(outer)
-        def _():
-            remote(z_mine.at[span(m)], z_in.at[span(m)], zs_in, zr_in.at[m], {"layer": z_inner}).start()
+        def send(r, k):
+            pl.when(outer)(lambda: remote(z_mine.at[r], z_in.at[r], zs_in, zr_in.at[k], {"layer": z_inner}).start())
+
+        by_parts(m, send)
+
+    def by_parts(m, act):
+        pl.when(m < ITEMS - 1)(lambda: act(span(m), m))
+
+        @pl.when(m == ITEMS - 1)
+        def _():
+            for i in range(SPLIT):
+                act(pl.ds((ITEMS - 1) * size + i * (size // SPLIT), size // SPLIT), ITEMS - 1 + i)
 
     def pair_up(m):
-        drain(z_in.at[span(m)], zr_in.at[m])
-        z_pair[span(m), :] = z_mine[span(m), :] + z_in[span(m), :]
-        remote(z_pair.at[span(m)], z_other.at[span(m)], zs_pair, zr_pair.at[m], {"layer": z_partner}).start()
+        def act(r, k):
+            drain(z_in.at[r], zr_in.at[k])
+            z_pair[r, :] = z_mine[r, :] + z_in[r, :]
+            remote(z_pair.at[r], z_other.at[r], zs_pair, zr_pair.at[k], {"layer": z_partner}).start()
+
+        by_parts(m, act)
 
     def unpack(t):
         q, p = place(t)
@@ -321,20 +350,24 @@
                 o_ref[span(4 * p + g), :] = block
             pltpu.make_async_copy(o_ref.at[whole(p)], o_hbm.at[whole(p)], out_sem).start()
 
+    def last(k):
+        return (k - ITEMS + PIECES + 1) * lax.div(k, ITEMS - PIECES)
+
     def finish(m):
-        drain(z_other.at[span(m)], zr_pair.at[m])
-        z_sum[span(m), :] = z_pair[span(m), :] + z_other[span(m), :]
-        remote(z_sum.at[span(m)], z_sum.at[span(m)], zs_out, zr_out.at[m], {"layer": z_outer}).start()
+        def act(r, k):
+            drain(z_other.at[r], zr_pair.at[k])
+            z_sum[r, :] = z_pair[r, :] + z_other[r, :]
+            remote(z_sum.at[r], z_sum.at[r], zs_out, zr_out.at[last(k)], {"layer": z_outer}).start()
+
+        by_parts(m, act)
         unpack(m)
 
     def run(stage, m):
         jax.named_scope(stage.__name__)(stage)(m)
 
     factor(0)
-    run(multiply, 0)
-    arrived(b_fars, 1)
-    exchange(1, 3)
-    run(multiply, 1)
+    lax.fori_loop(0, 2, lambda t, carry: (run(multiply, t), carry)[1], 0)
+
     exchange(2, 0)
     exchange(2, 1)
     arrived(seconds, 2)
@@ -375,7 +408,11 @@
         pl.when(t == 12)(lambda: factor(3))
         for stage, lag, least, cond in stages:
             m = t - lag
-            ok = jnp.logical_and(m >= least, m < ITEMS)
+            ok = t >= 0
+            for turn_at in SLOWER.get(stage.__name__, ()):
+                m += (t < turn_at).astype(jnp.int32)
+                ok = jnp.logical_and(ok, t != turn_at)
+            ok = jnp.logical_and(ok, jnp.logical_and(m >= least, m < ITEMS))
             if cond is not None:
                 ok = jnp.logical_and(ok, cond)
             pl.when(ok)(lambda stage=stage, m=m: run(stage, m))
@@ -387,11 +424,12 @@
         @pl.when(outer)
         def _():
             def take(m, carry):
-                drain(z_sum.at[span(m)], zr_out.at[m])
+                by_parts(m, lambda r, k: drain(z_sum.at[r], zr_out.at[last(k)]))
                 unpack(m)
                 return carry
 
-            lax.fori_loop(0, ITEMS, take, 0)
+            drain(z_sum.at[pl.ds(0, (ITEMS - PIECES) * size)], zr_out.at[0])
+            lax.fori_loop(ITEMS - PIECES, ITEMS, take, 0)
             drain(z_mine, zs_in)
 
         @pl.when(inner)
@@ -420,7 +458,7 @@
     both = pltpu.VMEM((ITEMS, 2, m // ITEMS // 2, BK), f32)
     late = pltpu.VMEM((m // 2, BK), f32)
     dma, regular = pltpu.SemaphoreType.DMA, pltpu.SemaphoreType.REGULAR
-    four, items = dma((4,)), dma((ITEMS,))
+    four, items, ends = dma((4,)), dma((ITEMS,)), dma((ITEMS - 1 + SPLIT,))
     return pl.pallas_call(
         kernel,
         out_shape=jax.ShapeDtypeStruct((m, BK), f32),
@@ -432,7 +470,7 @@
             both, both, both, both, late, late, late, late, whole, whole, whole, whole, whole,
             dma((2,)), dma, regular, regular, dma, dma, four, four, four,
             dma, dma, dma, dma, four, four, four, dma, four,
-            dma, dma, dma((ITEMS, 2)), dma, dma, items, dma, items, dma, items, dma, items,
+            dma, dma, items, dma, dma, items, dma, ends, dma, ends, dma, dma((PIECES + SPLIT,)),
         ],
         compiler_params=pltpu.CompilerParams(collective_id=0, has_side_effects=True, vmem_limit_bytes=52 * 2**20),
         name="panels_by_vectors",

time: 76.4 us -> 75.6 us (0.990)
  no operation moved by 1% of the time
where the time goes in v4:
time: 75.6 us; the launch traced here: 75.4 us
  Pallas kernels  73.5 us (97%)
  local copies, waits for them, and re-layouts  1.88 us (2%)
    pallas_call x1, Pallas kernels, local(): pl.pallas_call(kernel, out_shape=jax.ShapeDtypeStruct((m, BK), f32), in_s...  73.5 us
    unnamed x3, local copies, waits for them, and re-layouts  1.88 us

profile of v4, /device:TPU:24, one launch (start us, length us, event | category | flops | bytes accessed | tf_op | source)
XLA Modules:
  0.0 75.4 jit_solution(2568324113731502091)
XLA Ops:
  0.0 0.0 copy-start
  0.0 0.9 %copy-done = f32[256,128]{1,0:T(8,128)S(1)} copy-done((f32[256,128]{1,0:T(8,128)S(1)}, f32[256,128]{1,0:T(8,128)}, u32[]{:S(2)}) %copy-start) | copy-done | bytes 131096
  0.9 73.5 %panels_by_vectors.1 = f32[2048,128]{1,0:T(8,128)S(1)} custom-call(f32[2048,128]{1,0:T(8,128)} %a_hbm.1, f32[2,128,128]{2,1,0:T(8,128)S(1)} %bitcast.1), custom_call_target="tpu_custom_call" | custom-call | tf_op jit(solution)/shard_map/panels_by_vectors/pallas_call | solution.py:462
  74.4 1.0 %copy.4 = f32[2048,128]{1,0:T(8,128)} copy(f32[2048,128]{1,0:T(8,128)S(1)} %panels_by_vectors.1) | data formatting | bytes 2097152
Async XLA Ops:
  0.0 0.9 %copy-start = (f32[256,128]{1,0:T(8,128)S(1)}, f32[256,128]{1,0:T(8,128)}, u32[]{:S(2)}) copy-start(f32[256,128]{1,0:T(8,128)} %param.3) | copy-start | bytes 393220

commit v5 on v4

--- a/solution.py
+++ b/solution.py
@@ -11,8 +11,9 @@
 QUARTER = BK // QUARTERS
 PIECES = 4
 ITEMS = QUARTERS * PIECES
+RING = 8
 SPLIT = 4
-LAGS = (3, 6, 8, 11)
+LAGS = (3, 6, 7, 10)
 SLOWER = {"pass_on": (8,), "close_layer": (8, 10)}
 
 
@@ -304,18 +305,18 @@
         late_down[top(t), :] = below[part:]
         go_up[t, 0], go_up[t, 1] = far[:part], above[part:]
         go_down[t, 0], go_down[t, 1] = far[part:], below[:part]
-        remote(go_up.at[t], in_up.at[t], ps_up, pr.at[t], b_up).start()
-        remote(go_down.at[t], in_down.at[t], ps_down, pr.at[t], b_down).start()
+        remote(go_up.at[t], in_up.at[t], ps_up, pr.at[lax.rem(t, RING)], b_up).start()
+        remote(go_down.at[t], in_down.at[t], ps_down, pr.at[lax.rem(t, RING)], b_down).start()
 
     def pass_on(m):
-        drain(a_ref.at[pl.ds(0, 2 * size)], pr.at[m])
+        drain(a_ref.at[pl.ds(0, 2 * size)], pr.at[lax.rem(m, RING)])
         late_up[top(m), :] += in_up[m, 0]
-        remote(late_up.at[top(m)], end_up.at[top(m)], qs_up, qr.at[m], b_up).start()
+        remote(late_up.at[top(m)], end_up.at[top(m)], qs_up, qr.at[lax.rem(m, RING)], b_up).start()
         late_down[top(m), :] += in_down[m, 0]
-        remote(late_down.at[top(m)], end_down.at[top(m)], qs_down, qr.at[m], b_down).start()
+        remote(late_down.at[top(m)], end_down.at[top(m)], qs_down, qr.at[lax.rem(m, RING)], b_down).start()
 
     def close_layer(m):
-        drain(z_mine.at[span(m)], qr.at[m])
+        drain(z_mine.at[span(m)], qr.at[lax.rem(m, RING)])
         low, high = top(2 * m), top(2 * m + 1)
         z_mine[low, :] = keep[low, :] + (end_up[top(m), :] + in_down[m, 1])
         z_mine[high, :] = keep[high, :] + (in_up[m, 1] + end_down[top(m), :])
@@ -337,7 +338,7 @@
         def act(r, k):
             drain(z_in.at[r], zr_in.at[k])
             z_pair[r, :] = z_mine[r, :] + z_in[r, :]
-            remote(z_pair.at[r], z_other.at[r], zs_pair, zr_pair.at[k], {"layer": z_partner}).start()
+            remote(z_pair.at[r], z_other.at[r], zs_pair, zr_pair.at[lax.rem(k, ITEMS - 1 - RING + SPLIT)], {"layer": z_partner}).start()
 
         by_parts(m, act)
 
@@ -355,7 +356,7 @@
 
     def finish(m):
         def act(r, k):
-            drain(z_other.at[r], zr_pair.at[k])
+            drain(z_other.at[r], zr_pair.at[lax.rem(k, ITEMS - 1 - RING + SPLIT)])
             z_sum[r, :] = z_pair[r, :] + z_other[r, :]
             remote(z_sum.at[r], z_sum.at[r], zs_out, zr_out.at[last(k)], {"layer": z_outer}).start()
 
@@ -458,7 +459,7 @@
     both = pltpu.VMEM((ITEMS, 2, m // ITEMS // 2, BK), f32)
     late = pltpu.VMEM((m // 2, BK), f32)
     dma, regular = pltpu.SemaphoreType.DMA, pltpu.SemaphoreType.REGULAR
-    four, items, ends = dma((4,)), dma((ITEMS,)), dma((ITEMS - 1 + SPLIT,))
+    four, ring, ends = dma((4,)), dma((RING,)), dma((ITEMS - 1 + SPLIT,))
     return pl.pallas_call(
         kernel,
         out_shape=jax.ShapeDtypeStruct((m, BK), f32),
@@ -470,7 +471,7 @@
             both, both, both, both, late, late, late, late, whole, whole, whole, whole, whole,
             dma((2,)), dma, regular, regular, dma, dma, four, four, four,
             dma, dma, dma, dma, four, four, four, dma, four,
-            dma, dma, items, dma, dma, items, dma, ends, dma, ends, dma, dma((PIECES + SPLIT,)),
+            dma, dma, ring, dma, dma, ring, dma, ends, dma, dma((ITEMS - 1 - RING + SPLIT,)), dma, dma((PIECES + SPLIT,)),
         ],
         compiler_params=pltpu.CompilerParams(collective_id=0, has_side_effects=True, vmem_limit_bytes=52 * 2**20),
         name="panels_by_vectors",

time: 75.6 us -> 75.4 us (level)
  no operation moved by 1% of the time
where the time goes in v5:
time: 75.4 us; the launch traced here: 75.2 us
  Pallas kernels  73.3 us (97%)
  local copies, waits for them, and re-layouts  1.88 us (2%)
    pallas_call x1, Pallas kernels, local(): pl.pallas_call(kernel, out_shape=jax.ShapeDtypeStruct((m, BK), f32), in_s...  73.3 us
    unnamed x3, local copies, waits for them, and re-layouts  1.88 us

profile of v5, /device:TPU:24, one launch (start us, length us, event | category | flops | bytes accessed | tf_op | source)
XLA Modules:
  0.0 75.2 jit_solution(11325771133864392222)
XLA Ops:
  0.0 0.0 copy-start
  0.0 0.9 %copy-done = f32[256,128]{1,0:T(8,128)S(1)} copy-done((f32[256,128]{1,0:T(8,128)S(1)}, f32[256,128]{1,0:T(8,128)}, u32[]{:S(2)}) %copy-start) | copy-done | bytes 131096
  0.9 73.3 %panels_by_vectors.1 = f32[2048,128]{1,0:T(8,128)S(1)} custom-call(f32[2048,128]{1,0:T(8,128)} %a_hbm.1, f32[2,128,128]{2,1,0:T(8,128)S(1)} %bitcast.1), custom_call_target="tpu_custom_call" | custom-call | tf_op jit(solution)/shard_map/panels_by_vectors/pallas_call | solution.py:463
  74.2 1.0 %copy.4 = f32[2048,128]{1,0:T(8,128)} copy(f32[2048,128]{1,0:T(8,128)S(1)} %panels_by_vectors.1) | data formatting | bytes 2097152
Async XLA Ops:
  0.0 0.9 %copy-start = (f32[256,128]{1,0:T(8,128)S(1)}, f32[256,128]{1,0:T(8,128)}, u32[]{:S(2)}) copy-start(f32[256,128]{1,0:T(8,128)} %param.3) | copy-start | bytes 393220

commit v6 on v5

--- a/solution.py
+++ b/solution.py
@@ -207,6 +207,8 @@
 
     @pl.when(zh == 0)
     def _():
+        for q in range(1, QUARTERS):
+            exchange(q, 0)
         send_piece(2)
         send_piece(3)
         relay(0)
@@ -254,7 +256,7 @@
     arrived(b_fars, 0)
     exchange(0, 3)
     firsts[3].start()
-    exchange(1, 0)
+    pl.when(zh != 0)(lambda: exchange(1, 0))
     exchange(1, 1)
     take_piece(0)
     arrived(firsts, 2)
@@ -369,7 +371,7 @@
     factor(0)
     lax.fori_loop(0, 2, lambda t, carry: (run(multiply, t), carry)[1], 0)
 
-    exchange(2, 0)
+    pl.when(zh != 0)(lambda: exchange(2, 0))
     exchange(2, 1)
     arrived(seconds, 2)
     exchange(2, 2)
@@ -393,7 +395,7 @@
 
         @pl.when(t == 5)
         def _():
-            exchange(3, 0)
+            pl.when(zh != 0)(lambda: exchange(3, 0))
             exchange(3, 1)
 
         @pl.when(t == 6)

time: 75.4 us -> 77.7 us (1.031)
  Pallas kernels: 73.3 us -> 75.6 us
    pallas_call x1, Pallas kernels: 73.3 us -> 75.6 us  [local(): pl.pallas_call(kernel, out_shape=jax.ShapeDtypeStruct((m, BK), f32), in_s...]
where the time goes in v6:
time: 77.7 us; the launch traced here: 77.5 us
  Pallas kernels  75.6 us (97%)
  local copies, waits for them, and re-layouts  1.88 us (2%)
    pallas_call x1, Pallas kernels, local(): pl.pallas_call(kernel, out_shape=jax.ShapeDtypeStruct((m, BK), f32), in_s...  75.6 us
    unnamed x3, local copies, waits for them, and re-layouts  1.88 us

profile of v6, /device:TPU:24, one launch (start us, length us, event | category | flops | bytes accessed | tf_op | source)
XLA Modules:
  0.0 77.5 jit_solution(16690982070300401368)
XLA Ops:
  0.0 0.0 copy-start
  0.0 0.9 %copy-done = f32[256,128]{1,0:T(8,128)S(1)} copy-done((f32[256,128]{1,0:T(8,128)S(1)}, f32[256,128]{1,0:T(8,128)}, u32[]{:S(2)}) %copy-start) | copy-done | bytes 131096
  0.9 75.6 %panels_by_vectors.1 = f32[2048,128]{1,0:T(8,128)S(1)} custom-call(f32[2048,128]{1,0:T(8,128)} %a_hbm.1, f32[2,128,128]{2,1,0:T(8,128)S(1)} %bitcast.1), custom_call_target="tpu_custom_call" | custom-call | tf_op jit(solution)/shard_map/panels_by_vectors/pallas_call | solution.py:465
  76.5 1.0 %copy.4 = f32[2048,128]{1,0:T(8,128)} copy(f32[2048,128]{1,0:T(8,128)S(1)} %panels_by_vectors.1) | data formatting | bytes 2097152
Async XLA Ops:
  0.0 0.9 %copy-start = (f32[256,128]{1,0:T(8,128)S(1)}, f32[256,128]{1,0:T(8,128)}, u32[]{:S(2)}) copy-start(f32[256,128]{1,0:T(8,128)} %param.3) | copy-start | bytes 393220
